TPU v7x, 32 devices: a whole 2x2x4 slice. The times are simulated.
32 devices in a mesh: mom: 8 (over y, x, core), en: 4 (over z).
Axes of the slice: x: 2, y: 2, z: 4, core: 2. Of those that a mesh axis runs over, the one named last changes fastest.
Arguments:
- green: bfloat16 [2, 8, 16, 2, 128, 128], P(None, 'mom', 'en'), may hold values from -0.5 to 0.5
- bare: bfloat16 [2, 8, 16, 2, 128, 128], P(None, 'mom', 'en'), may hold values from -0.5 to 0.5
- coupling: bfloat16 [4, 128, 128], replicated, may hold values from -0.25 to 0.25
- occupation: float32 [4], replicated, may hold values from 0.2 to 2
- mode_shift: int32 [4], replicated, may hold values from -1 to 1, as said below
- mode_offset: int32 [4], replicated, may hold values from 1 to 4, as said below
- mode_block: int32 [2, 4], replicated, may hold values from 0 to 1
Outputs:
- updated: bfloat16 [2, 8, 16, 2, 128, 128], P(None, 'mom', 'en')
Inputs may be any that keep to these rules, and one draw needn't show every extreme that they name: `mode_shift`: each of -1, 0 and 1 is the shift of some mode. `mode_offset`: every offset from 1 to 4 is some mode's.
All inputs are finite; a program needn't handle non-finite values.
Results may differ from a plain program's by a relative error of at most 0.02.
Values may be sent and summed in bfloat16 or wider, within the bound.
A program may use at most 64 MiB of HBM per device.

v0:
```python
import functools

import jax
import jax.numpy as jnp
from jax import lax
from jax.experimental import pallas as pl
from jax.experimental.pallas import tpu as pltpu
from jax.sharding import PartitionSpec as P

MODES = 4
REACH = 4
PASSES = 2

RAW_UP, RAW_DOWN, RAW_NEXT, RAW_PREV, SHARE_NEXT, SHARE_PREV, PART_UP, PART_DOWN = range(8)
KINDS = 8

f32 = jnp.float32
bf16 = jnp.bfloat16


def matmul(left, right):
    return jnp.dot(left, right, preferred_element_type=f32)


def side_by_side(*parts):
    return parts[0] if len(parts) == 1 else jnp.concatenate(parts, axis=1)


def on_top(*parts):
    return parts[0] if len(parts) == 1 else jnp.concatenate(parts, axis=0)


def kernel(
    mom_count, en_count, passes,
    occupation_hbm, mode_shift_hbm, mode_offset_hbm, mode_block_hbm, green, bare_hbm, coupling_hbm,
    out,
    occupation, mode_shift, mode_offset, mode_block, bare, coupling, first_real,
    matrices, matrices_t, pair_t, wide_bare, real_coupled, below, above,
    share_own, part_own, real_current, low_rim, high_rim, imag_source,
    share_out, share_in, part_out, part_in, send_sem, recv_sem, green_sem, input_sem,
):
    energies = green.shape[2]
    blocks = green.shape[3]
    size = green.shape[4]
    k = lax.axis_index("mom")
    z = lax.axis_index("en")
    next_k = lax.rem(k + 1, mom_count)
    prev_k = lax.rem(k + mom_count - 1, mom_count)
    up_z = lax.rem(z + 1, en_count)
    down_z = lax.rem(z + en_count - 1, en_count)
    has_up = z < en_count - 1
    has_down = z > 0

    barrier = pltpu.get_barrier_semaphore()
    for other in (next_k, prev_k):
        pl.semaphore_signal(
            barrier, inc=1, device_id={"mom": other}, device_id_type=pl.DeviceIdType.MESH
        )

    @pl.when(has_up)
    def _():
        pl.semaphore_signal(
            barrier, inc=1, device_id={"en": up_z}, device_id_type=pl.DeviceIdType.MESH
        )

    @pl.when(has_down)
    def _():
        pl.semaphore_signal(
            barrier, inc=1, device_id={"en": down_z}, device_id_type=pl.DeviceIdType.MESH
        )

    middle = list(range(1, energies - 1))
    ends = [0, energies - 1]
    upward = list(range(energies))[::-1]
    downward = list(range(energies))

    real_fetch = [
        pltpu.make_async_copy(green.at[0, 0, e], first_real[e], green_sem.at[0, e])
        for e in range(energies)
    ]
    imag_fetch = [
        pltpu.make_async_copy(green.at[1, 0, e], imag_source[0][e].at[1], green_sem.at[1, e])
        for e in range(energies)
    ]
    pairs = (
        (coupling_hbm, coupling),
        (bare_hbm, bare),
        (occupation_hbm, occupation),
        (mode_shift_hbm, mode_shift),
        (mode_offset_hbm, mode_offset),
        (mode_block_hbm, mode_block),
    )
    input_fetch = [
        pltpu.make_async_copy(there, here, input_sem.at[i]) for i, (there, here) in enumerate(pairs)
    ]
    for e in ends + middle:
        imag_fetch[e].start()
        real_fetch[e].start()
    for fetch in input_fetch:
        fetch.start()

    pl.semaphore_wait(barrier, 2 + has_up.astype(jnp.int32) + has_down.astype(jnp.int32))

    def copy_of(p, kind, e):
        if kind == RAW_UP or kind == RAW_DOWN:
            source = first_real[e] if p == 0 else real_current[p - 1][e]
            target = low_rim[p][e] if kind == RAW_UP else high_rim[p][e]
        elif kind == RAW_NEXT or kind == RAW_PREV:
            source = imag_source[p][e].at[1]
            target = imag_source[p][e].at[2 if kind == RAW_NEXT else 0]
        elif kind == SHARE_NEXT or kind == SHARE_PREV:
            way = 1 if kind == SHARE_NEXT else 0
            source, target = share_out[p].at[way, e], share_in[p].at[way, e]
        else:
            way = 1 if kind == PART_UP else 0
            source, target = part_out[p].at[way, e], part_in[p].at[way, e]
        if kind in (RAW_NEXT, SHARE_NEXT):
            device = {"mom": next_k}
        elif kind in (RAW_PREV, SHARE_PREV):
            device = {"mom": prev_k}
        elif kind in (RAW_UP, PART_UP):
            device = {"en": up_z}
        else:
            device = {"en": down_z}
        return pltpu.make_async_remote_copy(
            src_ref=source,
            dst_ref=target,
            send_sem=send_sem.at[p, kind, e],
            recv_sem=recv_sem.at[p, kind, e],
            device_id=device,
            device_id_type=pl.DeviceIdType.MESH,
        )

    def guarded(condition, action):
        if condition is None:
            action()
        else:
            pl.when(condition)(action)

    def sends_if(kind):
        return {RAW_UP: has_up, PART_UP: has_up, RAW_DOWN: has_down, PART_DOWN: has_down}.get(kind)

    def receives_if(kind):
        return {RAW_UP: has_down, PART_UP: has_down, RAW_DOWN: has_up, PART_DOWN: has_up}.get(kind)

    def start(p, kind, e):
        guarded(sends_if(kind), lambda: copy_of(p, kind, e).start())

    waited = set()

    def arrived(p, kind, e):
        if (p, kind, e) not in waited:
            waited.add((p, kind, e))
            guarded(receives_if(kind), lambda: copy_of(p, kind, e).wait_recv())

    for i, e in enumerate(ends + middle):
        imag_fetch[e].wait()
        start(0, RAW_NEXT, e)
        start(0, RAW_PREV, e)
    for fetch in real_fetch:
        fetch.wait()
    for i in range(energies):
        start(0, RAW_UP, upward[i])
        start(0, RAW_DOWN, downward[i])

    @pl.when(jnp.logical_not(has_down))
    def _():
        for p in range(passes):
            for e in range(energies):
                low_rim[p][e][...] = jnp.zeros_like(low_rim[p][e])
            part_in[p][1] = jnp.zeros_like(part_in[p][1])

    @pl.when(jnp.logical_not(has_up))
    def _():
        for p in range(passes):
            for e in range(energies):
                high_rim[p][e][...] = jnp.zeros_like(high_rim[p][e])
            part_in[p][0] = jnp.zeros_like(part_in[p][0])

    for fetch in input_fetch:
        fetch.wait()

    weight, shift, picks = [], [], []
    for m in range(MODES):
        mode = jnp.int32(0)
        for j in range(1, MODES):
            mode = jnp.where(mode_offset[j] == m + 1, jnp.int32(j), mode)
        weight.append(occupation[mode])
        shift.append(mode_shift[mode])
        picks.append([mode_block[b, mode] for b in range(blocks)])
        matrix = coupling[mode]
        matrices[m] = matrix
        matrices_t[pl.ds(m * size, size), :] = matrix.astype(f32).T.astype(bf16)
    slot_of = []
    for q in (-1, 0, 1):
        slot = jnp.int32(0)
        for m in range(1, MODES):
            slot = jnp.where(shift[m] == q, jnp.int32(m), slot)
        slot_of.append(slot)
    extra = sum(range(MODES)) - slot_of[0] - slot_of[1] - slot_of[2]
    extra_shift = jnp.int32(0)
    for m in range(MODES):
        extra_shift = jnp.where(extra == m, shift[m], extra_shift)
    extra_t = matrices[extra].astype(f32).T
    for q in range(3):
        pair_t[q, pl.ds(0, size), :] = matrices[slot_of[q]].astype(f32).T.astype(bf16)
        kept = jnp.where(extra_shift == q - 1, 1.0, 0.0).astype(f32)
        pair_t[q, pl.ds(size, size), :] = (extra_t * kept).astype(bf16)

    for e in range(energies):
        for b in range(blocks):
            real, imag = bare[0, 0, e, b], bare[1, 0, e, b]
            wide_bare[e, b, pl.ds(0, size), :] = side_by_side(real, imag)
            wide_bare[e, b, pl.ds(size, size), :] = side_by_side(-imag, real)

    def real_at(p, e, pick):
        if e < 0:
            return low_rim[p][e + energies][pick]
        if e >= energies:
            return high_rim[p][e - energies][pick]
        return first_real[e][pick] if p == 0 else real_current[p - 1][e][pick]

    def imag_step(p, e):
        arrived(p, RAW_NEXT, e)
        arrived(p, RAW_PREV, e)
        for m in range(MODES):
            chosen = imag_source[p][e][shift[m] + 1]
            coupled = matmul(matrices[m], side_by_side(*[chosen[c] for c in range(blocks)]))
            lower = (weight[m] * coupled).astype(bf16)
            upper = ((weight[m] + 1.0) * coupled).astype(bf16)
            for c in range(blocks):
                below[e, m, c] = lower[:, c * size:(c + 1) * size]
                above[e, m, c] = upper[:, c * size:(c + 1) * size]

    def part_of(target):
        lower = [m for m in range(MODES) if 0 <= target - m - 1 < energies]
        upper = [m for m in range(MODES) if 0 <= target + m + 1 < energies]
        rows = []
        for b in range(blocks):
            terms = [below[target - m - 1, m, picks[m][b]] for m in lower]
            terms += [above[target + m + 1, m, picks[m][b]] for m in upper]
            rows.append(side_by_side(*terms))
        spans = [
            matrices_t[pl.ds(ms[0] * size, len(ms) * size), :] for ms in (lower, upper) if ms
        ]
        return matmul(on_top(*rows), on_top(*spans))

    def send_part(p, way, e):
        target = e + energies if way == 1 else e - energies
        part = part_of(target).astype(bf16)
        for b in range(blocks):
            part_out[p][way, e, b] = part[b * size:(b + 1) * size]
        start(p, PART_UP if way == 1 else PART_DOWN, e)

    def real_step(p, e):
        for m in range(MODES):
            for at in (e - m - 1, e + m + 1):
                if at < 0:
                    arrived(p, RAW_UP, at + energies)
                elif at >= energies:
                    arrived(p, RAW_DOWN, at - energies)
        for m in range(MODES):
            summed = []
            for b in range(blocks):
                low_side = real_at(p, e - m - 1, picks[m][b]).astype(f32)
                high_side = real_at(p, e + m + 1, picks[m][b]).astype(f32)
                mixed = weight[m] * low_side + (weight[m] + 1.0) * high_side
                summed.append(mixed.astype(bf16))
            coupled = matmul(matrices[m], side_by_side(*summed)).astype(bf16)
            for b in range(blocks):
                real_coupled[e, m, pl.ds(b * size, size), :] = coupled[:, b * size:(b + 1) * size]
        rest = real_coupled[e, extra]
        for q in (0, 2, 1):
            share = matmul(side_by_side(real_coupled[e, slot_of[q]], rest), pair_t[q])
            if q == 1:
                share_own[e] = share
            else:
                rounded = share.astype(bf16)
                way = 1 if q == 2 else 0
                for b in range(blocks):
                    share_out[p][way, e, b] = rounded[b * size:(b + 1) * size]
                start(p, SHARE_NEXT if way == 1 else SHARE_PREV, e)

    def close_step(p, e):
        for kind in (SHARE_NEXT, SHARE_PREV, PART_UP, PART_DOWN):
            arrived(p, kind, e)
        for b in range(blocks):
            rows = slice(b * size, (b + 1) * size)
            real = share_own[e, rows] + share_in[p][0, e, b].astype(f32)
            real = (real + share_in[p][1, e, b].astype(f32)).astype(bf16)
            imag = part_own[e, rows] + part_in[p][0, e, b].astype(f32)
            imag = (imag + part_in[p][1, e, b].astype(f32)).astype(bf16)
            sigma = on_top(side_by_side(real, imag), side_by_side(-imag, real))
            both = wide_bare[e, b, pl.ds(0, size), :]
            product = matmul(both, sigma).astype(bf16)
            new = (both.astype(f32) + matmul(product, wide_bare[e, b])).astype(bf16)
            if p == passes - 1:
                out[0, 0, e, b] = new[:, :size]
                out[1, 0, e, b] = new[:, size:]
            else:
                real_current[p][e][b] = new[:, :size]
                imag_source[p + 1][e][1, b] = new[:, size:]
        if p < passes - 1:
            start(p + 1, RAW_NEXT, e)
            start(p + 1, RAW_PREV, e)
            start(p + 1, RAW_UP, e)
            start(p + 1, RAW_DOWN, e)

    for p in range(passes):
        imag_order = ends + middle if p == 0 else middle + ends
        share_order = middle + ends
        shares, done, sent = list(share_order), set(), set()

        def ready_parts():
            found = []
            for i in range(energies):
                if all(j in done for j in range(i + 1)):
                    found.append((0, i))
                if all(j in done for j in range(energies - 1 - i, energies)):
                    found.append((1, energies - 1 - i))
            return [item for item in found if item not in sent]

        def send_next_part():
            way_and_energy = ready_parts()[0]
            sent.add(way_and_energy)
            send_part(p, *way_and_energy)

        for e in imag_order:
            if (p == 0 and e == imag_order[len(ends)]) or (p > 0 and e == imag_order[-1]):
                for _ in middle:
                    real_step(p, shares.pop(0))
            imag_step(p, e)
            done.add(e)
            if len(done) < energies:
                while ready_parts():
                    send_next_part()
        while ready_parts() or shares:
            if ready_parts():
                send_next_part()
            if shares and len(ready_parts()) % 2 == 0:
                real_step(p, shares.pop(0))
        for e in share_order:
            part_own[e] = part_of(e)
        for e in share_order:
            close_step(p, e)

    for p in range(passes):
        for kind in range(KINDS):
            def finish(p=p, kind=kind):
                for e in range(energies):
                    copy_of(p, kind, e).wait_send()

            guarded(sends_if(kind), finish)


def shards(mom_count, en_count, green, bare, coupling, occupation, mode_shift, mode_offset, mode_block):
    _, _, energies, blocks, size, _ = green.shape
    assert energies == REACH and coupling.shape[0] == MODES and MODES == REACH
    pair = (blocks, size, size)
    vmem = pltpu.VMEM
    smem = pltpu.SMEM
    scratch = [
        smem(occupation.shape, occupation.dtype),
        smem(mode_shift.shape, mode_shift.dtype),
        smem(mode_offset.shape, mode_offset.dtype),
        smem(mode_block.shape, mode_block.dtype),
        vmem(bare.shape, bf16),
        vmem(coupling.shape, bf16),
        [vmem(pair, bf16) for _ in range(energies)],
        vmem((MODES, size, size), bf16),
        vmem((MODES * size, size), bf16),
        vmem((3, 2 * size, size), bf16),
        vmem((energies, blocks, 2 * size, 2 * size), bf16),
        vmem((energies, MODES, blocks * size, size), bf16),
        vmem((energies, MODES) + pair, bf16),
        vmem((energies, MODES) + pair, bf16),
        vmem((energies, blocks * size, size), f32),
        vmem((energies, blocks * size, size), f32),
        [[vmem(pair, bf16) for _ in range(energies)] for _ in range(PASSES - 1)],
        [[vmem(pair, bf16) for _ in range(energies)] for _ in range(PASSES)],
        [[vmem(pair, bf16) for _ in range(energies)] for _ in range(PASSES)],
        [[vmem((3,) + pair, bf16) for _ in range(energies)] for _ in range(PASSES)],
        [vmem((2, energies) + pair, bf16) for _ in range(PASSES)],
        [vmem((2, energies) + pair, bf16) for _ in range(PASSES)],
        [vmem((2, energies) + pair, bf16) for _ in range(PASSES)],
        [vmem((2, energies) + pair, bf16) for _ in range(PASSES)],
        pltpu.SemaphoreType.DMA((PASSES, KINDS, energies)),
        pltpu.SemaphoreType.DMA((PASSES, KINDS, energies)),
        pltpu.SemaphoreType.DMA((2, energies)),
        pltpu.SemaphoreType.DMA((6,)),
    ]
    whole = pl.BlockSpec(memory_space=pltpu.VMEM)
    anywhere = pl.BlockSpec(memory_space=pltpu.HBM)
    return pl.pallas_call(
        functools.partial(kernel, mom_count, en_count, PASSES),
        out_shape=jax.ShapeDtypeStruct(green.shape, green.dtype),
        in_specs=[anywhere] * 7,
        out_specs=whole,
        scratch_shapes=scratch,
        compiler_params=pltpu.CompilerParams(
            collective_id=0, has_side_effects=True, vmem_limit_bytes=40 * 1024 * 1024
        ),
        name="born_passes",
    )(*[pltpu.with_memory_space_constraint(a, pltpu.HBM) for a in (occupation, mode_shift, mode_offset, mode_block, green, bare, coupling)])


def solution(mesh):
    spread = P(None, "mom", "en", None, None, None)
    return jax.shard_map(
        functools.partial(shards, mesh.shape["mom"], mesh.shape["en"]),
        mesh=mesh,
        in_specs=(spread, spread, P(), P(), P(), P(), P()),
        out_specs=spread,
        check_vma=False,
    )
```

profile of v0, /device:TPU:0, one launch (start us, length us, event | category | flops | bytes accessed | tf_op | source)
XLA Modules:
  0.0 34.8 jit_solution(7677456915687511336)
XLA Ops:
  0.0 34.0 %born_passes.1 = bf16[2,1,4,2,128,128]{5,4,3,2,1,0:T(8,128)(2,1)S(1)} custom-call(f32[4]{0:T(128)} %occupation_hbm.1, s32[4]{0:T(128)} %mode_shift_hbm.1, s32[4]{0:T(128)} %mode_offset_hbm.1, s32[2,4]{1,0:T(2,128)} %mode_block_hbm.1, bf16[2,1,4,2,128,128]{5,4,3,2,1,0:T(8,128)(2,1)} %green.1, bf16[2,1,4,2,128,128]{5,4,3,2,1,0:T(8,128)(2,1)} %bare_hbm.1, ...), custom_call_target="tpu_custom_call" | custom-call | tf_op jit(solution)/shard_map/born_passes/pallas_call | solution.py:394
  34.0 0.8 %copy.9 = bf16[2,1,4,2,128,128]{5,4,3,2,1,0:T(8,128)(2,1)} copy(bf16[2,1,4,2,128,128]{5,4,3,2,1,0:T(8,128)(2,1)S(1)} %born_passes.1) | data formatting | bytes 1048576
where the time goes:
time: 35 us; the launch traced here: 34.8 us
  Pallas kernels  34 us (97%)
  local copies, waits for them, and re-layouts  0.8 us (2%)
    pallas_call x1, Pallas kernels, shards(): pl.pallas_call(functools.partial(kernel, mom_count, en_count, PASSES), ou...  34 us
    unnamed x1, local copies, waits for them, and re-layouts  0.8 us

commit v1 on v0

v1 whole, which is shorter than its diff:
```python
import functools

import jax
import jax.numpy as jnp
from jax import lax
from jax.experimental import pallas as pl
from jax.experimental.pallas import tpu as pltpu
from jax.sharding import PartitionSpec as P

MODES = 4
REACH = 4
PASSES = 2

FROM_NEXT, FROM_PREV, FROM_DOWN, FROM_UP = range(4)
OWN = 2

f32 = jnp.float32
bf16 = jnp.bfloat16

UPWARD = ((3, 2, 1, 0), (1, 3, 2, 0))
DOWNWARD = ((0, 1, 2, 3), (1, 0, 3, 2))
ACROSS = ((3, 0, 2, 1), (1, 0, 3, 2))

STEPS = (
    (
    (
        "Q10+Q20", "I3+U3", "Q11+Q00", "I0+D0", "Q21+Q30+Q12+Q01", "I2+U2", "Q22+Q31+Q13+S1", "Q02+Q03+S0",
        "I1+D1+U1", "Q23+Q32+U0+D3", "Q33+S3+D2", "S2", "O1+A1+O0+A0", "O3+A3+O2+A2", "C1", "C0", "C3", "C2",
    ),
    (
        "Q10+Q20", "Q02", "I1+Q13+Q31", "Q11+Q00+Q22", "I0+D0+D1", "Q21+Q30", "Q12+S1+Q01", "I3+U3", "Q33",
        "Q03+S0", "I2+U1+D3", "Q23+Q32+S3+U0", "S2+U2+D2", "O1+A1+O0+A0", "O3+A3+O2+A2", "C1", "C0", "C3",
        "C2",
    ),
    ),
    (
    (
        "Q10+Q20", "Q11+Q00", "Q21+Q30+Q12+Q01", "Q22+Q31", "I3+U3", "Q13+S1", "Q23+Q32", "I0+D0",
        "Q02+Q03+S0", "Q33+S3", "I2+U2+S2", "I1+D1+U1", "D3+U0", "D2", "O1+A1+O0+A0", "O3+A3+O2+A2", "C1",
        "C0", "C3", "C2",
    ),
    (
        "Q10+Q20", "Q02", "I1+Q13+Q31", "Q11+Q00+Q22", "I0+D0+D1", "Q21+Q30", "Q12+S1+Q01", "I3+U3", "Q33",
        "Q03+S0", "I2+U1+D3", "Q23+Q32+S3+U0", "S2+U2+D2", "O1+A1+O0+A0", "O3+A3+O2+A2", "C1", "C0", "C3",
        "C2",
    ),
    ),
)


def matmul(left, right):
    return jnp.dot(left, right, preferred_element_type=f32)


def side_by_side(*parts):
    return parts[0] if len(parts) == 1 else jnp.concatenate(parts, axis=1)


def on_top(*parts):
    return parts[0] if len(parts) == 1 else jnp.concatenate(parts, axis=0)


def kernel(
    mom_count, en_count, passes,
    occupation_hbm, mode_shift_hbm, mode_offset_hbm, mode_block_hbm, green, bare_hbm, coupling_hbm,
    out,
    occupation, mode_shift, mode_offset, mode_block, bare, coupling,
    matrices, matrices_t, share_t, own_t, wide_bare, real_coupled, below, above,
    share_own, part_own, real_current, low_rim, high_rim, imag_source,
    share_out, part_out, inbox,
    rim_sem, imag_sem, inbox_sem, send_sem, input_sem,
):
    energies = green.shape[2]
    blocks = green.shape[3]
    size = green.shape[4]
    k = lax.axis_index("mom")
    z = lax.axis_index("en")
    next_k = lax.rem(k + 1, mom_count)
    prev_k = lax.rem(k + mom_count - 1, mom_count)
    up_z = lax.rem(z + 1, en_count)
    down_z = lax.rem(z + en_count - 1, en_count)
    is_odd = lax.rem(k, 2) == 1
    is_even = lax.rem(k, 2) == 0
    has_up = z < en_count - 1
    has_down = z > 0

    barrier = pltpu.get_barrier_semaphore()
    for other in (next_k, prev_k):
        pl.semaphore_signal(
            barrier, inc=1, device_id={"mom": other}, device_id_type=pl.DeviceIdType.MESH
        )

    @pl.when(has_up)
    def _():
        pl.semaphore_signal(
            barrier, inc=1, device_id={"en": up_z}, device_id_type=pl.DeviceIdType.MESH
        )

    @pl.when(has_down)
    def _():
        pl.semaphore_signal(
            barrier, inc=1, device_id={"en": down_z}, device_id_type=pl.DeviceIdType.MESH
        )

    pairs = (
        (coupling_hbm, coupling),
        (bare_hbm, bare),
        (occupation_hbm, occupation),
        (mode_shift_hbm, mode_shift),
        (mode_offset_hbm, mode_offset),
        (mode_block_hbm, mode_block),
    )
    input_fetch = [
        pltpu.make_async_copy(there, here, input_sem.at[i]) for i, (there, here) in enumerate(pairs)
    ]
    green_fetch = [
        pltpu.make_async_copy(green.at[0, 0, e], real_current[0][e], input_sem.at[len(pairs)])
        for e in range(energies)
    ]
    green_fetch += [
        pltpu.make_async_copy(green.at[1, 0, e], imag_source[0][e].at[OWN], input_sem.at[len(pairs)])
        for e in range(energies)
    ]
    for fetch in green_fetch + input_fetch:
        fetch.start()

    pl.semaphore_wait(barrier, 2 + has_up.astype(jnp.int32) + has_down.astype(jnp.int32))

    pltpu.make_async_copy(bare, bare, input_sem.at[len(pairs)]).wait()

    def send(source, target, sent, landed, device):
        pltpu.make_async_remote_copy(
            src_ref=source,
            dst_ref=target,
            send_sem=sent,
            recv_sem=landed,
            device_id=device,
            device_id_type=pl.DeviceIdType.MESH,
        ).start()

    def across(source, targets, landed):
        return [
            lambda: send(source[0], targets[0], send_sem.at[0], landed, {"mom": next_k}),
            lambda: send(source[1], targets[1], send_sem.at[0], landed, {"mom": prev_k}),
        ]

    def imag_across(p, e):
        source = imag_source[p][e].at[OWN]
        slots = imag_source[p][e]
        return across((source, source), (slots.at[1], slots.at[0]), imag_sem.at[p, e])

    def start(actions):
        for action in actions:
            action()

    def send_up(source, target, landed):
        send(source, target, send_sem.at[1], landed, {"en": up_z})

    def send_down(source, target, landed):
        send(source, target, send_sem.at[2], landed, {"en": down_z})

    def send_real_up(p, e):
        send_up(real_current[p][e], low_rim[p][e], rim_sem.at[p, 0, e])

    def send_real_down(p, e):
        send_down(real_current[p][e], high_rim[p][e], rim_sem.at[p, 1, e])

    first = [imag_across(0, e) for e in ACROSS[0]]
    pl.when(is_odd)(lambda: start([ways[0] for ways in first]))
    pl.when(is_even)(lambda: start([ways[1] for ways in first]))
    pl.when(has_up)(lambda: [send_real_up(0, e) for e in UPWARD[0]] and None)
    pl.when(has_down)(lambda: [send_real_down(0, e) for e in DOWNWARD[0]] and None)
    pl.when(is_odd)(lambda: start([ways[1] for ways in first]))
    pl.when(is_even)(lambda: start([ways[0] for ways in first]))

    @pl.when(jnp.logical_not(has_down))
    def _():
        for p in range(passes):
            for j in range(energies):
                low_rim[p][j][...] = jnp.zeros_like(low_rim[p][j])
                inbox[p, j, FROM_DOWN] = jnp.zeros_like(inbox[p, j, FROM_DOWN])

    @pl.when(jnp.logical_not(has_up))
    def _():
        for p in range(passes):
            for j in range(energies):
                high_rim[p][j][...] = jnp.zeros_like(high_rim[p][j])
                inbox[p, j, FROM_UP] = jnp.zeros_like(inbox[p, j, FROM_UP])

    for fetch in input_fetch:
        fetch.wait()

    weight, shift, slot, picks = [], [], [], []
    for m in range(MODES):
        mode = jnp.int32(0)
        for j in range(1, MODES):
            mode = jnp.where(mode_offset[j] == m + 1, jnp.int32(j), mode)
        weight.append(occupation[mode])
        shift.append(mode_shift[mode])
        slot.append(jnp.where(shift[m] == 0, OWN, jnp.where(shift[m] > 0, 1, 0)))
        picks.append([mode_block[b, mode] for b in range(blocks)])
        matrix = coupling[mode]
        turned = matrix.astype(f32).T
        rows = pl.ds(m * size, size)
        matrices[m] = matrix
        matrices_t[rows, :] = turned.astype(bf16)
        for q, (kept_t, columns) in {
            1: (share_t, pl.ds(0, size)), -1: (share_t, pl.ds(size, size)), 0: (own_t, pl.ds(0, size)),
        }.items():
            kept = jnp.where(shift[m] == q, 1.0, 0.0).astype(f32)
            kept_t[rows, columns] = (turned * kept).astype(bf16)

    for e in range(energies):
        for b in range(blocks):
            real, imag = bare[0, 0, e, b], bare[1, 0, e, b]
            wide_bare[e, b, pl.ds(0, size), :] = side_by_side(real, imag)
            wide_bare[e, b, pl.ds(size, size), :] = side_by_side(-imag, real)

    waited, sends, closed = set(), [], []

    def in_turn(order, ready):
        return next((i for i, e in enumerate(order) if e not in ready), len(order))

    def later(condition, action):
        sends.append((condition, action))

    def later_across(ways):
        far, near = (0, 1) if parity else (1, 0)
        later("far", ways[far])
        later("near", ways[near])

    def send_all():
        for condition, guard in (("far", None), (has_up, has_up), (has_down, has_down), ("near", None)):
            actions = [action for wanted, action in sends if wanted is condition]
            if actions and guard is None:
                start(actions)
            elif actions:
                pl.when(guard)(functools.partial(start, actions))
        sends.clear()

    def landed_pair(sem, both, one):
        pl.when(jnp.logical_and(has_up, has_down))(lambda: pltpu.make_async_copy(both, both, sem).wait())
        pl.when(jnp.logical_xor(has_up, has_down))(lambda: pltpu.make_async_copy(one, one, sem).wait())

    def once(*key):
        fresh = key not in waited
        waited.add(key)
        return fresh

    def rim_landed(p, side, e):
        if once("rim", p, side, e):
            one = (low_rim, high_rim)[side][p][e]
            pl.when((has_down, has_up)[side])(lambda: pltpu.make_async_copy(one, one, rim_sem.at[p, side, e]).wait())

    def imag_landed(p, e):
        if once("imag", p, e):
            both = imag_source[p][e].at[pl.ds(0, 2)]
            pltpu.make_async_copy(both, both, imag_sem.at[p, e]).wait()

    def inbox_landed(p, e):
        if once("inbox", p, e):
            landed_pair(inbox_sem.at[p, e], inbox.at[p, e], inbox.at[p, e, pl.ds(0, 3)])

    def real_at(p, e, pick):
        if e < 0:
            return low_rim[p][e + energies][pick]
        if e >= energies:
            return high_rim[p][e - energies][pick]
        return real_current[p][e][pick]

    def rims_landed(p, e, m):
        if e - m - 1 < 0:
            rim_landed(p, 0, e - m - 1 + energies)
        if e + m + 1 >= energies:
            rim_landed(p, 1, e + m + 1 - energies)

    def mode_step(p, e, m):
        summed = []
        for b in range(blocks):
            low_side = real_at(p, e - m - 1, picks[m][b]).astype(f32)
            high_side = real_at(p, e + m + 1, picks[m][b]).astype(f32)
            mixed = weight[m] * low_side + (weight[m] + 1.0) * high_side
            summed.append(mixed.astype(bf16))
        coupled = matmul(matrices[m], side_by_side(*summed)).astype(bf16)
        for b in range(blocks):
            real_coupled[e, pl.ds(b * size, size), pl.ds(m * size, size)] = coupled[:, b * size:(b + 1) * size]

    def share_step(p, e):
        share = matmul(real_coupled[e], share_t[...]).astype(bf16)
        for way in range(2):
            for b in range(blocks):
                share_out[p][e, way, b] = share[b * size:(b + 1) * size, way * size:(way + 1) * size]
        later_across(across(
            (share_out[p].at[e, 0], share_out[p].at[e, 1]),
            (inbox.at[p, e, FROM_PREV], inbox.at[p, e, FROM_NEXT]), inbox_sem.at[p, e],
        ))

    def own_share_step(p, e):
        share_own[e] = matmul(real_coupled[e], own_t[...])

    def imag_step(p, e):
        for m in range(MODES):
            chosen = imag_source[p][e][slot[m]]
            coupled = matmul(matrices[m], side_by_side(*[chosen[c] for c in range(blocks)]))
            lower = (weight[m] * coupled).astype(bf16)
            upper = ((weight[m] + 1.0) * coupled).astype(bf16)
            for c in range(blocks):
                below[e, m, c] = lower[:, c * size:(c + 1) * size]
                above[e, m, c] = upper[:, c * size:(c + 1) * size]

    def part_of(target):
        lower = [m for m in range(MODES) if 0 <= target - m - 1 < energies]
        upper = [m for m in range(MODES) if 0 <= target + m + 1 < energies]
        rows = []
        for b in range(blocks):
            terms = [below[target - m - 1, m, picks[m][b]] for m in lower]
            terms += [above[target + m + 1, m, picks[m][b]] for m in upper]
            rows.append(side_by_side(*terms))
        spans = [
            matrices_t[pl.ds(ms[0] * size, len(ms) * size), :] for ms in (lower, upper) if ms
        ]
        return matmul(on_top(*rows), on_top(*spans))

    def part_step(p, e, up):
        part = part_of(e + energies if up else e - energies).astype(bf16)
        source = part_out[p].at[1 if up else 0, e]
        for b in range(blocks):
            part_out[p][1 if up else 0, e, b] = part[b * size:(b + 1) * size]
        if up:
            later(has_up, lambda: send_up(source, inbox.at[p, e, FROM_DOWN], inbox_sem.at[p, e]))
        else:
            later(has_down, lambda: send_down(source, inbox.at[p, e, FROM_UP], inbox_sem.at[p, e]))

    def own_part_step(p, e):
        part_own[e] = part_of(e)

    def close_step(p, e):
        for b in range(blocks):
            rows = slice(b * size, (b + 1) * size)
            real = share_own[e, rows] + inbox[p, e, FROM_NEXT, b].astype(f32)
            real = (real + inbox[p, e, FROM_PREV, b].astype(f32)).astype(bf16)
            imag = part_own[e, rows] + inbox[p, e, FROM_DOWN, b].astype(f32)
            imag = (imag + inbox[p, e, FROM_UP, b].astype(f32)).astype(bf16)
            sigma = on_top(side_by_side(real, imag), side_by_side(-imag, real))
            both = wide_bare[e, b, pl.ds(0, size), :]
            product = matmul(both, sigma).astype(bf16)
            new = (both.astype(f32) + matmul(product, wide_bare[e, b])).astype(bf16)
            if p == passes - 1:
                out[0, 0, e, b] = new[:, :size]
                out[1, 0, e, b] = new[:, size:]
            else:
                real_current[p + 1][e][b] = new[:, :size]
                imag_source[p + 1][e][OWN, b] = new[:, size:]
        if p < passes - 1:
            closed.append(e)
            for condition, order, action in ((None, ACROSS, imag_across), (has_up, UPWARD, send_real_up), (has_down, DOWNWARD, send_real_down)):
                begin, end = in_turn(order[p + 1], closed[:-1]), in_turn(order[p + 1], closed)
                for turn in order[p + 1][begin:end]:
                    if condition is None:
                        later_across(action(p + 1, turn))
                    else:
                        later(condition, functools.partial(action, p + 1, turn))

    steps = {
        "Q": mode_step, "S": share_step, "O": own_share_step, "I": imag_step,
        "U": functools.partial(part_step, up=True), "D": functools.partial(part_step, up=False),
        "A": own_part_step, "C": close_step,
    }
    waits = {"Q": rims_landed, "I": imag_landed, "C": inbox_landed}
    def run(odd):
        nonlocal parity
        parity = odd
        waited.clear()
        for p in range(passes):
            closed.clear()
            for group in STEPS[odd][p]:
                calls = [(name[0], [int(digit) for digit in name[1:]]) for name in group.split("+")]
                for kind, at in calls:
                    if kind in waits:
                        waits[kind](p, *at)
                for kind, at in calls:
                    steps[kind](p, *at)
                send_all()

    parity = 0
    pl.when(is_even)(lambda: run(0))
    pl.when(is_odd)(lambda: run(1))

    everything = inbox.at[0]
    pltpu.make_async_copy(inbox, inbox, send_sem.at[0]).wait()
    pl.when(has_up)(lambda: pltpu.make_async_copy(everything, everything, send_sem.at[1]).wait())
    pl.when(has_down)(lambda: pltpu.make_async_copy(everything, everything, send_sem.at[2]).wait())


def shards(mom_count, en_count, green, bare, coupling, occupation, mode_shift, mode_offset, mode_block):
    _, _, energies, blocks, size, _ = green.shape
    assert energies == REACH and coupling.shape[0] == MODES and MODES == REACH
    pair = (blocks, size, size)
    vmem = pltpu.VMEM
    smem = pltpu.SMEM
    dma = pltpu.SemaphoreType.DMA
    scratch = [
        smem(occupation.shape, occupation.dtype),
        smem(mode_shift.shape, mode_shift.dtype),
        smem(mode_offset.shape, mode_offset.dtype),
        smem(mode_block.shape, mode_block.dtype),
        vmem(bare.shape, bf16),
        vmem(coupling.shape, bf16),
        vmem((MODES, size, size), bf16),
        vmem((MODES * size, size), bf16),
        vmem((MODES * size, 2 * size), bf16),
        vmem((MODES * size, size), bf16),
        vmem((energies, blocks, 2 * size, 2 * size), bf16),
        vmem((energies, blocks * size, MODES * size), bf16),
        vmem((energies, MODES) + pair, bf16),
        vmem((energies, MODES) + pair, bf16),
        vmem((energies, blocks * size, size), f32),
        vmem((energies, blocks * size, size), f32),
        [[vmem(pair, bf16) for _ in range(energies)] for _ in range(PASSES)],
        [[vmem(pair, bf16) for _ in range(energies)] for _ in range(PASSES)],
        [[vmem(pair, bf16) for _ in range(energies)] for _ in range(PASSES)],
        [[vmem((3,) + pair, bf16) for _ in range(energies)] for _ in range(PASSES)],
        [vmem((energies, 2) + pair, bf16) for _ in range(PASSES)],
        [vmem((2, energies) + pair, bf16) for _ in range(PASSES)],
        vmem((PASSES, energies, 4) + pair, bf16),
        dma((PASSES, 2, energies)),
        dma((PASSES, energies)),
        dma((PASSES, energies)),
        dma((3,)),
        dma((7,)),
    ]
    whole = pl.BlockSpec(memory_space=pltpu.VMEM)
    anywhere = pl.BlockSpec(memory_space=pltpu.HBM)
    return pl.pallas_call(
        functools.partial(kernel, mom_count, en_count, PASSES),
        out_shape=jax.ShapeDtypeStruct(green.shape, green.dtype),
        in_specs=[anywhere] * 7,
        out_specs=whole,
        scratch_shapes=scratch,
        compiler_params=pltpu.CompilerParams(
            collective_id=0, has_side_effects=True, vmem_limit_bytes=40 * 1024 * 1024
        ),
        name="born_passes",
    )(*[pltpu.with_memory_space_constraint(a, pltpu.HBM) for a in (occupation, mode_shift, mode_offset, mode_block, green, bare, coupling)])


def solution(mesh):
    spread = P(None, "mom", "en", None, None, None)
    return jax.shard_map(
        functools.partial(shards, mesh.shape["mom"], mesh.shape["en"]),
        mesh=mesh,
        in_specs=(spread, spread, P(), P(), P(), P(), P()),
        out_specs=spread,
        check_vma=False,
    )
```

time: 35 us -> 31.9 us (0.911)
  Pallas kernels: 34 us -> 31 us
    pallas_call x1, Pallas kernels: 34 us -> 31 us  [shards(): pl.pallas_call(functools.partial(kernel, mom_count, en_count, PASSES), ou...]
where the time goes in v1:
time: 31.9 us; the launch traced here: 31.8 us
  Pallas kernels  31 us (97%)
  local copies, waits for them, and re-layouts  0.8 us (3%)
    pallas_call x1, Pallas kernels, shards(): pl.pallas_call(functools.partial(kernel, mom_count, en_count, PASSES), ou...  31 us
    unnamed x1, local copies, waits for them, and re-layouts  0.8 us

profile of v1, /device:TPU:0, one launch (start us, length us, event | category | flops | bytes accessed | tf_op | source)
XLA Modules:
  0.0 31.8 jit_solution(9347741909194694395)
XLA Ops:
  0.0 31.0 %born_passes.1 = bf16[2,1,4,2,128,128]{5,4,3,2,1,0:T(8,128)(2,1)S(1)} custom-call(f32[4]{0:T(128)} %occupation_hbm.1, s32[4]{0:T(128)} %mode_shift_hbm.1, s32[4]{0:T(128)} %mode_offset_hbm.1, s32[2,4]{1,0:T(2,128)} %mode_block_hbm.1, bf16[2,1,4,2,128,128]{5,4,3,2,1,0:T(8,128)(2,1)} %green.1, bf16[2,1,4,2,128,128]{5,4,3,2,1,0:T(8,128)(2,1)} %bare_hbm.1, ...), custom_call_target="tpu_custom_call" | custom-call | tf_op jit(solution)/shard_map/born_passes/pallas_call | solution.py:434
  31.0 0.8 %copy.9 = bf16[2,1,4,2,128,128]{5,4,3,2,1,0:T(8,128)(2,1)} copy(bf16[2,1,4,2,128,128]{5,4,3,2,1,0:T(8,128)(2,1)S(1)} %born_passes.1) | data formatting | bytes 1048576

commit v2 on v1

--- a/solution.py
+++ b/solution.py
@@ -24,28 +24,32 @@
 STEPS = (
     (
     (
-        "Q10+Q20", "I3+U3", "Q11+Q00", "I0+D0", "Q21+Q30+Q12+Q01", "I2+U2", "Q22+Q31+Q13+S1", "Q02+Q03+S0",
-        "I1+D1+U1", "Q23+Q32+U0+D3", "Q33+S3+D2", "S2", "O1+A1+O0+A0", "O3+A3+O2+A2", "C1", "C0", "C3", "C2",
-    ),
-    (
-        "Q10+Q20", "Q02", "I1+Q13+Q31", "Q11+Q00+Q22", "I0+D0+D1", "Q21+Q30", "Q12+S1+Q01", "I3+U3", "Q33",
-        "Q03+S0", "I2+U1+D3", "Q23+Q32+S3+U0", "S2+U2+D2", "O1+A1+O0+A0", "O3+A3+O2+A2", "C1", "C0", "C3",
-        "C2",
-    ),
-    ),
-    (
-    (
-        "Q10+Q20", "Q11+Q00", "Q21+Q30+Q12+Q01", "Q22+Q31", "I3+U3", "Q13+S1", "Q23+Q32", "I0+D0",
-        "Q02+Q03+S0", "Q33+S3", "I2+U2+S2", "I1+D1+U1", "D3+U0", "D2", "O1+A1+O0+A0", "O3+A3+O2+A2", "C1",
-        "C0", "C3", "C2",
-    ),
-    (
-        "Q10+Q20", "Q02", "I1+Q13+Q31", "Q11+Q00+Q22", "I0+D0+D1", "Q21+Q30", "Q12+S1+Q01", "I3+U3", "Q33",
-        "Q03+S0", "I2+U1+D3", "Q23+Q32+S3+U0", "S2+U2+D2", "O1+A1+O0+A0", "O3+A3+O2+A2", "C1", "C0", "C3",
-        "C2",
+        "Q10+Q20", "J33+U3", "J30+J31+J32", "Q11+Q00", "J03+D0", "J00+J01+J02+Q21+Q30+Q12+Q01", "I2",
+        "Q13+S1", "J13+D1+U1", "Q22+Q31+J10+J11+J12+Q02+Q03+S0+U0+D3", "Q32+Q33+S3", "Q23+S2+D2+U2",
+        "O1+A1+O0+A0", "O3+A3+O2+A2", "C10", "C11", "C0", "C3", "C2",
+    ),
+    (
+        "Q10+Q20", "Q02", "I1", "Q13+Q31", "J02+J03+D0+D1", "J00+J01+Q11+Q00+Q22", "Q12+S1", "J33+U3",
+        "J30+J31+J32+Q21+Q30+Q01+Q33+Q03+S0", "J22+J23+U1+D3+D2", "J20+J21+Q23+Q32+S3+U0", "S2+U2",
+        "O1+A1+O0+A0", "O3+A3+O2+A2", "C1", "C0", "C3", "C2",
+    ),
+    ),
+    (
+    (
+        "Q10+Q20", "Q11+Q00", "Q21+Q30+Q12+Q01", "J33+U3", "J30+J31+J32+Q13+S1", "Q22+Q31", "J03+D0",
+        "J00+J01+J02+Q02+Q03+S0", "Q23+Q32", "I2", "Q33+S3", "J13+D1+U1", "J10+J11+J12+S2+D3+U0", "D2+U2",
+        "O1+A1+O0+A0", "O3+A3+O2+A2", "C10", "C11", "C0", "C3", "C2",
+    ),
+    (
+        "Q10+Q20", "Q02", "I1", "Q13+Q31", "J02+J03+D0+D1", "J00+J01+Q11+Q00+Q22", "Q12+S1", "J33+U3",
+        "J30+J31+J32+Q21+Q30+Q01+Q33+Q03+S0", "J22+J23+U1+D3+D2", "J20+J21+Q23+Q32+S3+U0", "S2+U2",
+        "O1+A1+O0+A0", "O3+A3+O2+A2", "C1", "C0", "C3", "C2",
     ),
     ),
 )
+
+
+HALVED = ((1,), ())
 
 
 def matmul(left, right):
@@ -144,10 +148,20 @@
             lambda: send(source[1], targets[1], send_sem.at[0], landed, {"mom": prev_k}),
         ]
 
-    def imag_across(p, e):
-        source = imag_source[p][e].at[OWN]
-        slots = imag_source[p][e]
-        return across((source, source), (slots.at[1], slots.at[0]), imag_sem.at[p, e])
+    def imag_across(p, e, rows=slice(None)):
+        source = part_ref(imag_source[p][e].at[OWN], rows)
+        targets = part_ref(imag_source[p][e].at[1], rows), part_ref(imag_source[p][e].at[0], rows)
+        return across((source, source), targets, imag_sem.at[p, e])
+
+    def part_ref(ref, rows):
+        return ref if rows == slice(None) else ref.at[rows]
+
+    def pieces(p, e):
+        return [slice(b, b + 1) for b in range(blocks)] if e in HALVED[p] else [slice(None)]
+
+    def inbox_landing(p, e, piece):
+        extra = [(q, x) for q in range(passes) for x in HALVED[q]]
+        return inbox_sem.at[passes * energies + extra.index((p, e)) if piece else p * energies + e]
 
     def start(actions):
         for action in actions:
@@ -159,11 +173,11 @@
     def send_down(source, target, landed):
         send(source, target, send_sem.at[2], landed, {"en": down_z})
 
-    def send_real_up(p, e):
-        send_up(real_current[p][e], low_rim[p][e], rim_sem.at[p, 0, e])
-
-    def send_real_down(p, e):
-        send_down(real_current[p][e], high_rim[p][e], rim_sem.at[p, 1, e])
+    def send_real_up(p, e, rows=slice(None)):
+        send_up(part_ref(real_current[p][e], rows), part_ref(low_rim[p][e], rows), rim_sem.at[p, 0, e])
+
+    def send_real_down(p, e, rows=slice(None)):
+        send_down(part_ref(real_current[p][e], rows), part_ref(high_rim[p][e], rows), rim_sem.at[p, 1, e])
 
     first = [imag_across(0, e) for e in ACROSS[0]]
     pl.when(is_odd)(lambda: start([ways[0] for ways in first]))
@@ -252,14 +266,18 @@
             one = (low_rim, high_rim)[side][p][e]
             pl.when((has_down, has_up)[side])(lambda: pltpu.make_async_copy(one, one, rim_sem.at[p, side, e]).wait())
 
-    def imag_landed(p, e):
+    def imag_landed(p, e, m=None):
         if once("imag", p, e):
             both = imag_source[p][e].at[pl.ds(0, 2)]
             pltpu.make_async_copy(both, both, imag_sem.at[p, e]).wait()
 
-    def inbox_landed(p, e):
-        if once("inbox", p, e):
-            landed_pair(inbox_sem.at[p, e], inbox.at[p, e], inbox.at[p, e, pl.ds(0, 3)])
+    def inbox_landed(p, e, piece=0):
+        rows = pieces(p, e)[piece]
+        landed_pair(
+            inbox_landing(p, e, piece),
+            inbox.at[p, e, :, rows] if rows != slice(None) else inbox.at[p, e],
+            inbox.at[p, e, pl.ds(0, 3), rows] if rows != slice(None) else inbox.at[p, e, pl.ds(0, 3)],
+        )
 
     def real_at(p, e, pick):
         if e < 0:
@@ -290,23 +308,28 @@
         for way in range(2):
             for b in range(blocks):
                 share_out[p][e, way, b] = share[b * size:(b + 1) * size, way * size:(way + 1) * size]
-        later_across(across(
-            (share_out[p].at[e, 0], share_out[p].at[e, 1]),
-            (inbox.at[p, e, FROM_PREV], inbox.at[p, e, FROM_NEXT]), inbox_sem.at[p, e],
-        ))
+        for piece, rows in enumerate(pieces(p, e)):
+            later_across(across(
+                (part_ref(share_out[p].at[e, 0], rows), part_ref(share_out[p].at[e, 1], rows)),
+                (part_ref(inbox.at[p, e, FROM_PREV], rows), part_ref(inbox.at[p, e, FROM_NEXT], rows)),
+                inbox_landing(p, e, piece),
+            ))
 
     def own_share_step(p, e):
         share_own[e] = matmul(real_coupled[e], own_t[...])
 
+    def imag_mode_step(p, e, m):
+        chosen = imag_source[p][e][slot[m]]
+        coupled = matmul(matrices[m], side_by_side(*[chosen[c] for c in range(blocks)]))
+        lower = (weight[m] * coupled).astype(bf16)
+        upper = ((weight[m] + 1.0) * coupled).astype(bf16)
+        for c in range(blocks):
+            below[e, m, c] = lower[:, c * size:(c + 1) * size]
+            above[e, m, c] = upper[:, c * size:(c + 1) * size]
+
     def imag_step(p, e):
         for m in range(MODES):
-            chosen = imag_source[p][e][slot[m]]
-            coupled = matmul(matrices[m], side_by_side(*[chosen[c] for c in range(blocks)]))
-            lower = (weight[m] * coupled).astype(bf16)
-            upper = ((weight[m] + 1.0) * coupled).astype(bf16)
-            for c in range(blocks):
-                below[e, m, c] = lower[:, c * size:(c + 1) * size]
-                above[e, m, c] = upper[:, c * size:(c + 1) * size]
+            imag_mode_step(p, e, m)
 
     def part_of(target):
         lower = [m for m in range(MODES) if 0 <= target - m - 1 < energies]
@@ -326,16 +349,18 @@
         source = part_out[p].at[1 if up else 0, e]
         for b in range(blocks):
             part_out[p][1 if up else 0, e, b] = part[b * size:(b + 1) * size]
-        if up:
-            later(has_up, lambda: send_up(source, inbox.at[p, e, FROM_DOWN], inbox_sem.at[p, e]))
-        else:
-            later(has_down, lambda: send_down(source, inbox.at[p, e, FROM_UP], inbox_sem.at[p, e]))
+        condition, send_part, place = (has_up, send_up, FROM_DOWN) if up else (has_down, send_down, FROM_UP)
+        for piece, rows in enumerate(pieces(p, e)):
+            later(condition, functools.partial(
+                send_part, part_ref(source, rows), part_ref(inbox.at[p, e, place], rows), inbox_landing(p, e, piece)
+            ))
 
     def own_part_step(p, e):
         part_own[e] = part_of(e)
 
-    def close_step(p, e):
-        for b in range(blocks):
+    def close_step(p, e, piece=0):
+        halved = e in HALVED[p]
+        for b in [piece] if halved else range(blocks):
             rows = slice(b * size, (b + 1) * size)
             real = share_own[e, rows] + inbox[p, e, FROM_NEXT, b].astype(f32)
             real = (real + inbox[p, e, FROM_PREV, b].astype(f32)).astype(bf16)
@@ -351,22 +376,31 @@
             else:
                 real_current[p + 1][e][b] = new[:, :size]
                 imag_source[p + 1][e][OWN, b] = new[:, size:]
-        if p < passes - 1:
-            closed.append(e)
-            for condition, order, action in ((None, ACROSS, imag_across), (has_up, UPWARD, send_real_up), (has_down, DOWNWARD, send_real_down)):
-                begin, end = in_turn(order[p + 1], closed[:-1]), in_turn(order[p + 1], closed)
-                for turn in order[p + 1][begin:end]:
-                    if condition is None:
-                        later_across(action(p + 1, turn))
-                    else:
-                        later(condition, functools.partial(action, p + 1, turn))
+        if p == passes - 1:
+            return
+        if halved:
+            rows = pieces(p, e)[piece]
+            later_across(imag_across(p + 1, e, rows))
+            later(has_up, functools.partial(send_real_up, p + 1, e, rows))
+            later(has_down, functools.partial(send_real_down, p + 1, e, rows))
+            if piece == 0:
+                closed.append(e)
+            return
+        closed.append(e)
+        for condition, order, action in ((None, ACROSS, imag_across), (has_up, UPWARD, send_real_up), (has_down, DOWNWARD, send_real_down)):
+            begin, end = in_turn(order[p + 1], closed[:-1]), in_turn(order[p + 1], closed)
+            for turn in order[p + 1][begin:end]:
+                if condition is None:
+                    later_across(action(p + 1, turn))
+                else:
+                    later(condition, functools.partial(action, p + 1, turn))
 
     steps = {
-        "Q": mode_step, "S": share_step, "O": own_share_step, "I": imag_step,
+        "Q": mode_step, "S": share_step, "O": own_share_step, "I": imag_step, "J": imag_mode_step,
         "U": functools.partial(part_step, up=True), "D": functools.partial(part_step, up=False),
         "A": own_part_step, "C": close_step,
     }
-    waits = {"Q": rims_landed, "I": imag_landed, "C": inbox_landed}
+    waits = {"Q": rims_landed, "I": imag_landed, "J": imag_landed, "C": inbox_landed}
     def run(odd):
         nonlocal parity
         parity = odd
@@ -425,7 +459,7 @@
         vmem((PASSES, energies, 4) + pair, bf16),
         dma((PASSES, 2, energies)),
         dma((PASSES, energies)),
-        dma((PASSES, energies)),
+        dma((PASSES * energies + sum(map(len, HALVED)),)),
         dma((3,)),
         dma((7,)),
     ]

time: 31.9 us -> 31.2 us (0.978)
  Pallas kernels: 31 us -> 30.3 us
    pallas_call x1, Pallas kernels: 31 us -> 30.3 us  [shards(): pl.pallas_call(functools.partial(kernel, mom_count, en_count, PASSES), ou...]
where the time goes in v2:
time: 31.2 us; the launch traced here: 31.1 us
  Pallas kernels  30.3 us (97%)
  local copies, waits for them, and re-layouts  0.8 us (3%)
    pallas_call x1, Pallas kernels, shards(): pl.pallas_call(functools.partial(kernel, mom_count, en_count, PASSES), ou...  30.3 us
    unnamed x1, local copies, waits for them, and re-layouts  0.8 us

profile of v2, /device:TPU:0, one launch (start us, length us, event | category | flops | bytes accessed | tf_op | source)
XLA Modules:
  0.0 31.1 jit_solution(17949119884768235316)
XLA Ops:
  0.0 30.3 %born_passes.1 = bf16[2,1,4,2,128,128]{5,4,3,2,1,0:T(8,128)(2,1)S(1)} custom-call(f32[4]{0:T(128)} %occupation_hbm.1, s32[4]{0:T(128)} %mode_shift_hbm.1, s32[4]{0:T(128)} %mode_offset_hbm.1, s32[2,4]{1,0:T(2,128)} %mode_block_hbm.1, bf16[2,1,4,2,128,128]{5,4,3,2,1,0:T(8,128)(2,1)} %green.1, bf16[2,1,4,2,128,128]{5,4,3,2,1,0:T(8,128)(2,1)} %bare_hbm.1, ...), custom_call_target="tpu_custom_call" | custom-call | tf_op jit(solution)/shard_map/born_passes/pallas_call | solution.py:468
  30.3 0.8 %copy.9 = bf16[2,1,4,2,128,128]{5,4,3,2,1,0:T(8,128)(2,1)} copy(bf16[2,1,4,2,128,128]{5,4,3,2,1,0:T(8,128)(2,1)S(1)} %born_passes.1) | data formatting | bytes 1048576

commit v3 on v2

--- a/solution.py
+++ b/solution.py
@@ -29,8 +29,8 @@
         "O1+A1+O0+A0", "O3+A3+O2+A2", "C10", "C11", "C0", "C3", "C2",
     ),
     (
-        "Q10+Q20", "Q02", "I1", "Q13+Q31", "J02+J03+D0+D1", "J00+J01+Q11+Q00+Q22", "Q12+S1", "J33+U3",
-        "J30+J31+J32+Q21+Q30+Q01+Q33+Q03+S0", "J22+J23+U1+D3+D2", "J20+J21+Q23+Q32+S3+U0", "S2+U2",
+        "Q10+Q20", "Q02", "I1", "Q13+Q31", "J02+J03+D0+D1", "J00+J01+Q11+Q00+Q22", "Q12+S1", "Q01", "J33+U3",
+        "J30+J31+J32+Q03+S0", "Q21+Q30+Q33", "J22+J23+U1+D3+D2", "J20+J21+Q23+Q32+S3+U0", "S2+U2",
         "O1+A1+O0+A0", "O3+A3+O2+A2", "C1", "C0", "C3", "C2",
     ),
     ),
@@ -41,8 +41,8 @@
         "O1+A1+O0+A0", "O3+A3+O2+A2", "C10", "C11", "C0", "C3", "C2",
     ),
     (
-        "Q10+Q20", "Q02", "I1", "Q13+Q31", "J02+J03+D0+D1", "J00+J01+Q11+Q00+Q22", "Q12+S1", "J33+U3",
-        "J30+J31+J32+Q21+Q30+Q01+Q33+Q03+S0", "J22+J23+U1+D3+D2", "J20+J21+Q23+Q32+S3+U0", "S2+U2",
+        "Q10+Q20", "Q02", "I1", "Q13+Q31", "J02+J03+D0+D1", "J00+J01+Q11+Q00+Q22", "Q12+S1", "Q01", "J33+U3",
+        "J30+J31+J32+Q03+S0", "Q21+Q30+Q33", "J22+J23+U1+D3+D2", "J20+J21+Q23+Q32+S3+U0", "S2+U2",
         "O1+A1+O0+A0", "O3+A3+O2+A2", "C1", "C0", "C3", "C2",
     ),
     ),
@@ -50,6 +50,10 @@
 
 
 HALVED = ((1,), ())
+
+IMAG_SLOT = ((0, 1, 2, 3), (0, 3, 1, 2))
+LOW_SLOT = ((0, 1, 2, 3), (0, 3, 1, 2))
+HIGH_SLOT = ((0, 1, 2, 3), (1, 0, 2, 4))
 
 
 def matmul(left, right):
@@ -108,7 +112,6 @@
 
     pairs = (
         (coupling_hbm, coupling),
-        (bare_hbm, bare),
         (occupation_hbm, occupation),
         (mode_shift_hbm, mode_shift),
         (mode_offset_hbm, mode_offset),
@@ -125,12 +128,13 @@
         pltpu.make_async_copy(green.at[1, 0, e], imag_source[0][e].at[OWN], input_sem.at[len(pairs)])
         for e in range(energies)
     ]
+    green_fetch += [pltpu.make_async_copy(bare_hbm, bare, input_sem.at[len(pairs)])]
     for fetch in green_fetch + input_fetch:
         fetch.start()
 
     pl.semaphore_wait(barrier, 2 + has_up.astype(jnp.int32) + has_down.astype(jnp.int32))
 
-    pltpu.make_async_copy(bare, bare, input_sem.at[len(pairs)]).wait()
+    pltpu.make_async_copy(inbox.at[0], inbox.at[0], input_sem.at[len(pairs)]).wait()
 
     def send(source, target, sent, landed, device):
         pltpu.make_async_remote_copy(
@@ -151,7 +155,7 @@
     def imag_across(p, e, rows=slice(None)):
         source = part_ref(imag_source[p][e].at[OWN], rows)
         targets = part_ref(imag_source[p][e].at[1], rows), part_ref(imag_source[p][e].at[0], rows)
-        return across((source, source), targets, imag_sem.at[p, e])
+        return across((source, source), targets, imag_sem.at[IMAG_SLOT[p][e]])
 
     def part_ref(ref, rows):
         return ref if rows == slice(None) else ref.at[rows]
@@ -174,10 +178,10 @@
         send(source, target, send_sem.at[2], landed, {"en": down_z})
 
     def send_real_up(p, e, rows=slice(None)):
-        send_up(part_ref(real_current[p][e], rows), part_ref(low_rim[p][e], rows), rim_sem.at[p, 0, e])
+        send_up(part_ref(real_current[p][e], rows), part_ref(low_rim[p][e], rows), rim_sem.at[0, LOW_SLOT[p][e]])
 
     def send_real_down(p, e, rows=slice(None)):
-        send_down(part_ref(real_current[p][e], rows), part_ref(high_rim[p][e], rows), rim_sem.at[p, 1, e])
+        send_down(part_ref(real_current[p][e], rows), part_ref(high_rim[p][e], rows), rim_sem.at[1, HIGH_SLOT[p][e]])
 
     first = [imag_across(0, e) for e in ACROSS[0]]
     pl.when(is_odd)(lambda: start([ways[0] for ways in first]))
@@ -264,12 +268,12 @@
     def rim_landed(p, side, e):
         if once("rim", p, side, e):
             one = (low_rim, high_rim)[side][p][e]
-            pl.when((has_down, has_up)[side])(lambda: pltpu.make_async_copy(one, one, rim_sem.at[p, side, e]).wait())
+            pl.when((has_down, has_up)[side])(lambda: pltpu.make_async_copy(one, one, rim_sem.at[side, (LOW_SLOT, HIGH_SLOT)[side][p][e]]).wait())
 
     def imag_landed(p, e, m=None):
         if once("imag", p, e):
             both = imag_source[p][e].at[pl.ds(0, 2)]
-            pltpu.make_async_copy(both, both, imag_sem.at[p, e]).wait()
+            pltpu.make_async_copy(both, both, imag_sem.at[IMAG_SLOT[p][e]]).wait()
 
     def inbox_landed(p, e, piece=0):
         rows = pieces(p, e)[piece]
@@ -457,11 +461,11 @@
         [vmem((energies, 2) + pair, bf16) for _ in range(PASSES)],
         [vmem((2, energies) + pair, bf16) for _ in range(PASSES)],
         vmem((PASSES, energies, 4) + pair, bf16),
-        dma((PASSES, 2, energies)),
-        dma((PASSES, energies)),
+        dma((2, REACH + 1)),
+        dma((REACH,)),
         dma((PASSES * energies + sum(map(len, HALVED)),)),
         dma((3,)),
-        dma((7,)),
+        dma((6,)),
     ]
     whole = pl.BlockSpec(memory_space=pltpu.VMEM)
     anywhere = pl.BlockSpec(memory_space=pltpu.HBM)

time: 31.2 us -> 31.2 us (level)
  no operation moved by 1% of the time
where the time goes in v3:
time: 31.2 us; the launch traced here: 31.1 us
  Pallas kernels  30.3 us (97%)
  local copies, waits for them, and re-layouts  0.8 us (3%)
    pallas_call x1, Pallas kernels, shards(): pl.pallas_call(functools.partial(kernel, mom_count, en_count, PASSES), ou...  30.3 us
    unnamed x1, local copies, waits for them, and re-layouts  0.8 us

profile of v3, /device:TPU:0, one launch (start us, length us, event | category | flops | bytes accessed | tf_op | source)
XLA Modules:
  0.0 31.1 jit_solution(8781682728370168569)
XLA Ops:
  0.0 30.3 %born_passes.1 = bf16[2,1,4,2,128,128]{5,4,3,2,1,0:T(8,128)(2,1)S(1)} custom-call(f32[4]{0:T(128)} %occupation_hbm.1, s32[4]{0:T(128)} %mode_shift_hbm.1, s32[4]{0:T(128)} %mode_offset_hbm.1, s32[2,4]{1,0:T(2,128)} %mode_block_hbm.1, bf16[2,1,4,2,128,128]{5,4,3,2,1,0:T(8,128)(2,1)} %green.1, bf16[2,1,4,2,128,128]{5,4,3,2,1,0:T(8,128)(2,1)} %bare_hbm.1, ...), custom_call_target="tpu_custom_call" | custom-call | tf_op jit(solution)/shard_map/born_passes/pallas_call | solution.py:472
  30.3 0.8 %copy.9 = bf16[2,1,4,2,128,128]{5,4,3,2,1,0:T(8,128)(2,1)} copy(bf16[2,1,4,2,128,128]{5,4,3,2,1,0:T(8,128)(2,1)S(1)} %born_passes.1) | data formatting | bytes 1048576
